TPU v7x, 256 devices: a whole 4x4x8 slice. The times are simulated.
256 devices in a mesh: section: 2 (over core), dp: 16 (over z, x_lo), tensor: 8 (over y, x_hi).
Axes of the slice: x: 4 (x_hi: 2, x_lo: 2; x = x_hi * 2 + x_lo), y: 4, z: 8, core: 2. Of those that a mesh axis runs over, the one named last changes fastest.
Arguments:
- tokens: bfloat16 [2048, 4096], P('dp', 'tensor'), may hold values from -6 to 6
- gain: bfloat16 [2, 4096], P('section', 'tensor'), may hold values from 0.099609375 to 1.8984375
- w_up: bfloat16 [2, 4096, 5120], P('section', 'dp', 'tensor'), may hold values from -0.09375 to 0.09375
- w_down: bfloat16 [2, 5120, 4096], P('section', 'tensor', 'dp'), may hold values from -0.078125 to 0.078125
- cotangent: bfloat16 [2, 2048, 4096], P('section', 'dp'), may hold values from -6 to 6
Outputs:
- states: bfloat16 [2, 2048, 4096], P('section', 'dp', 'tensor')
- grad_down: bfloat16 [2, 5120, 4096], P('section', 'tensor', 'dp')
All inputs are finite; a program needn't handle non-finite values.
Results may differ from a plain program's by a relative error of at most 0.02.
Values may be sent and summed in bfloat16 or wider, within the bound.
No kernel may reach another device: no remote copies, remote signals or barrier semaphores. Data moves between devices by JAX's collectives and lax.ppermute only.
A program may use at most 64 MiB of HBM per device.

v0:
```python
import jax
import jax.numpy as jnp
from jax import lax
from jax.sharding import Mesh
from jax.sharding import PartitionSpec as P

MICRO = 2
MB_ROWS = 64
DP = ("dp_0", "dp_1")
EPS = 1e-06


def gathered_by_axis(array, axes, dim):
    filled = array
    for number in range(len(axes) - 1, -1, -1):
        filled = lax.all_gather(filled, axes[number], axis=dim, tiled=True)
    return filled


def in_order(pieces, dim):
    dims = list(pieces.shape[1:])
    dims[dim] *= pieces.shape[0]
    return jnp.moveaxis(pieces, 0, dim).reshape(dims)


def copy_for_each(array, axis):
    peers = lax.axis_size(axis)
    return lax.all_to_all(
        jnp.broadcast_to(array[None], (peers, *array.shape)), axis, 0, 0, tiled=True
    )


def collect(array, axis, dim):
    return in_order(copy_for_each(array, axis), dim)


def split_up(array, dim, peers):
    before, after = (array.shape[:dim], array.shape[dim + 1 :])
    return jnp.moveaxis(array.reshape(*before, peers, -1, *after), dim, 0)


def summed_on_arrival(array, axis, dim):
    pieces = split_up(array, dim, lax.axis_size(axis))
    arrived = lax.all_to_all(pieces, axis, split_axis=0, concat_axis=0, tiled=True)
    return arrived.astype(jnp.float32).sum(axis=0)


def shifted(array, axis, by):
    peers = lax.axis_size(axis)
    pairs = [(i, i + by) for i in range(peers) if 0 <= i + by < peers]
    return lax.ppermute(array, axis, pairs)


def body(tokens, gain, w_up, w_down, cotangent):
    section_id = lax.axis_index("section")
    section_count = lax.axis_size("section")
    up_whole = gathered_by_axis(w_up[0], DP, 0)
    down_whole = gathered_by_axis(w_down[0], DP, 1)
    width = up_whole.shape[0]
    hidden_width = up_whole.shape[1]
    gain_own = gain[0]
    gain_whole = lax.all_gather(gain_own, "tensor", axis=0, tiled=True)
    micro_rows = MB_ROWS
    micro_count = MICRO
    own_width = tokens.shape[1]
    tok_rows = tokens.shape[0]

    def project(normed):
        pre_act = jnp.dot(normed, up_whole, preferred_element_type=jnp.float32)
        hidden = jax.nn.gelu(pre_act, approximate=True).astype(jnp.bfloat16)
        partial_value = jnp.dot(hidden, down_whole, preferred_element_type=jnp.float32).astype(
            jnp.bfloat16
        )
        return (hidden, lax.optimization_barrier(partial_value).astype(jnp.float32))

    def skipped(normed):
        return (
            jnp.zeros((micro_rows, hidden_width), jnp.bfloat16),
            jnp.zeros((micro_rows, width), jnp.float32),
        )

    def advance(step_id, loop_state):
        incoming, states, hiddens = loop_state
        micro_id = step_id - section_id
        active = (micro_id >= 0) & (micro_id < micro_count)
        slot_pos = jnp.clip(micro_id, 0, micro_count - 1) * micro_rows
        entry_rows = lax.dynamic_slice_in_dim(tokens, slot_pos, micro_rows, 0)
        current = jnp.where(section_id == 0, entry_rows, incoming)
        current_f = current.astype(jnp.float32)
        whole_rows = collect(current, "tensor", 1)
        whole_f = whole_rows.astype(jnp.float32)
        inverse_rms = lax.rsqrt(jnp.mean(whole_f * whole_f, axis=1, keepdims=True) + EPS)
        normed = (whole_f * inverse_rms * gain_whole.astype(jnp.float32)).astype(jnp.bfloat16)
        hidden, partial_value = lax.cond(active, project, skipped, normed)
        summed = summed_on_arrival(partial_value.astype(jnp.bfloat16), "tensor", 1)
        result = (current_f + summed).astype(jnp.bfloat16)
        old_state = lax.dynamic_slice_in_dim(states, slot_pos, micro_rows, 0)
        states = lax.dynamic_update_slice_in_dim(
            states, jnp.where(active, result, old_state), slot_pos, 0
        )
        old_hidden = lax.dynamic_slice_in_dim(hiddens, slot_pos, micro_rows, 0)
        hiddens = lax.dynamic_update_slice_in_dim(
            hiddens, jnp.where(active, hidden, old_hidden), slot_pos, 0
        )
        incoming = shifted(result, "section", 1)
        return (incoming, states, hiddens)

    initial = (
        jnp.zeros((micro_rows, own_width), jnp.bfloat16),
        jnp.zeros((tok_rows, own_width), jnp.bfloat16),
        jnp.zeros((tok_rows, hidden_width), jnp.bfloat16),
    )
    final_state = lax.fori_loop(0, micro_count + section_count - 1, advance, initial)
    states = final_state[1]
    hiddens = final_state[2]
    cot_own = cotangent[0]
    dp_count = lax.axis_size(DP)
    hidden_all = lax.all_gather(hiddens, DP, axis=0, tiled=True)
    cot_mine = lax.all_to_all(cot_own, DP, split_axis=1, concat_axis=0, tiled=True)
    grad_own = jnp.zeros((hidden_width, width // dp_count), jnp.float32)
    for peer_id in range(dp_count):
        lower = peer_id * tok_rows
        partial_value = lax.dot_general(
            hidden_all[lower : lower + tok_rows],
            cot_mine[lower : lower + tok_rows],
            (((0,), (0,)), ((), ())),
            preferred_element_type=jnp.float32,
        ).astype(jnp.bfloat16)
        grad_own = grad_own + lax.optimization_barrier(partial_value).astype(jnp.float32)
    return (states[None], grad_own.astype(jnp.bfloat16)[None])


def solution(mesh):
    torus = Mesh(
        mesh.devices.reshape(mesh.shape["section"], 8, 2, mesh.shape["tensor"]),
        ("section", "dp_0", "dp_1", "tensor"),
    )
    in_specs = (
        P(DP, "tensor"),
        P("section", "tensor"),
        P("section", DP, "tensor"),
        P("section", "tensor", DP),
        P("section", DP, None),
    )
    out_specs = (P("section", DP, "tensor"), P("section", "tensor", DP))
    return jax.shard_map(body, mesh=torus, in_specs=in_specs, out_specs=out_specs, check_vma=False)
```

profile of v0, /device:TPU:2, one launch (start us, length us, event | category | flops | bytes accessed | tf_op | source)
XLA Modules:
  0.0 377.0 jit_solution(14900252217565980653)
XLA Ops:
  7.2 10.4 %all-gather.1 = bf16[1,512,640]{2,1,0:T(8,128)(2,1)} all-gather(bf16[1,256,640]{2,1,0:T(8,128)(2,1)} %param.11), channel_id=3, replica_groups=mesh['section'=2,'dp_0'=8,'dp_1'=2,'tensor'=8] {'dp_1'}, dimensions={1}, use_global_device_ids=true | all-gather | bytes 983040 | tf_op jit(solution)/shard_map/all_gather | solution.py:16
  17.7 11.1 %all-gather.3 = bf16[1,640,512]{2,1,0:T(8,128)(2,1)} all-gather(bf16[1,640,256]{2,1,0:T(8,128)(2,1)} %param.12), channel_id=5, replica_groups=mesh['section'=2,'dp_0'=8,'dp_1'=2,'tensor'=8] {'dp_1'}, dimensions={2}, use_global_device_ids=true | all-gather | bytes 983040 | tf_op jit(solution)/shard_map/all_gather | solution.py:16
  29.0 31.6 %all-gather = bf16[1,4096]{1,0:T(2,128)(2,1)S(1)} all-gather(bf16[1,512]{1,0:T(2,128)(2,1)S(1)} %copy-done.7), channel_id=2, replica_groups=mesh['section'=2,'dp_0'=8,'dp_1'=2,'tensor'=8] {'tensor'}, dimensions={1}, use_global_device_ids=true | all-gather | bytes 9216 | tf_op jit(solution)/shard_map/all_gather | solution.py:62
  60.6 25.8 %all-gather.11.cloned.1.call-done = bf16[1,4096,640]{2,1,0:T(8,128)(2,1)} async-done(((bf16[1,512,640]{2,1,0:T(8,128)(2,1)}), bf16[1,4096,640]{2,1,0:T(8,128)(2,1)}) %all-gather.11.cloned.1.call-update) | async-done | bytes 5242896 | tf_op jit(solution)/shard_map/all_gather | solution.py:16
  86.5 65.0 %all-gather.13.cloned.1.call-done = bf16[1,640,4096]{2,1,0:T(8,128)(2,1)} async-done(((bf16[1,640,512]{2,1,0:T(8,128)(2,1)}), bf16[1,640,4096]{2,1,0:T(8,128)(2,1)}) %all-gather.13.cloned.1.call-update) | async-done | bytes 5242896 | tf_op jit(solution)/shard_map/all_gather | solution.py:16
  151.6 124.7 %while.18 = (s32[]{:T(128)}, bf16[64,512]{1,0:T(8,128)(2,1)S(1)}, bf16[128,512]{1,0:T(8,128)(2,1)S(1)}, bf16[128,640]{1,0:T(8,128)(2,1)S(1)}, pred[]{:T(512)}, /...) while((s32[]{:T(128)}, bf16[64,512]{1,0:T(8,128)(2,1)S(1)}, ...), condition=%wide.region_5.6_spmd, body=%wide.region_0.5_spmd.sunk | while | flops 674254912 | bytes 67036620 | solution.py:113
  151.6 0.8 broadcast_in_dim.44
  152.5 5.8 %all-to-all-start = ((bf16[8,64,512]{2,1,0:T(8,128)(2,1)}), bf16[8,64,512]{2,1,0:T(8,128)(2,1)S(1)}, u32[]{:S(2)}, u32[]{:S(2)}) async-start(bf16[8,64,512]{2,1,0:T(8,128)(2,1)} %broadcast_in_dim.44), calls=%async_computation | async-start | bytes 1048576 | tf_op jit(solution)/shard_map/while/body/eval_jaxpr/all_to_all | solution.py:28
  158.3 11.4 %all-to-all-done = bf16[8,64,512]{2,1,0:T(8,128)(2,1)S(1)} async-done(((bf16[8,64,512]{2,1,0:T(8,128)(2,1)}), bf16[8,64,512]{2,1,0:T(8,128)(2,1)S(1)}, u32[]{:S(2)}, u32[]{:S(2)}) %all-to-all-start) | async-done | bytes 524320 | tf_op jit(solution)/shard_map/while/body/eval_jaxpr/all_to_all | solution.py:28
  170.3 2.1 copy-done
  172.4 4.5 %conditional.2 = (bf16[64,640]{1,0:T(8,128)(2,1)}, bf16[64,4096]{1,0:T(8,128)(2,1)S(1)}) conditional(s32[]{:T(128)} %convert_element_type.313, () %tuple.49, (bf16[64,4096]{1,0:T(8,128)(2,1)S(1)}, bf16[4096,640]{1,0:T(8,128)(2,1)S(1)}, bf16[640,4096]{1,0:T(8,128)(2,1)}) %tuple.63), branch_computations={%region_2.2_spmd, %region_3.3_spmd} | conditional | flops 671719424 | bytes 32669740 | solution.py:94
  172.4 1.7 fusion.7
  174.1 0.9 copy-done.1
  174.9 1.9 convolution_convert_fusion
  177.1 1.0 copy.67
  178.0 3.5 all-to-all-start.1
  181.5 10.1 %all-to-all-done.1 = bf16[8,64,512]{2,1,0:T(8,128)(2,1)S(1)} async-done(((bf16[8,64,512]{2,1,0:T(8,128)(2,1)}), bf16[8,64,512]{2,1,0:T(8,128)(2,1)S(1)}, u32[]{:S(2)}, u32[]{:S(2)}) %all-to-all-start.1) | async-done | bytes 524320 | tf_op jit(solution)/shard_map/while/body/eval_jaxpr/all_to_all | solution.py:44
  191.7 1.3 collective-permute-start
  193.0 0.9 select_dynamic-update-slice_fusion.5
  194.0 0.8 broadcast_in_dim.44
  194.9 3.5 all-to-all-start
  198.4 12.2 %all-to-all-done = bf16[8,64,512]{2,1,0:T(8,128)(2,1)S(1)} async-done(((bf16[8,64,512]{2,1,0:T(8,128)(2,1)}), bf16[8,64,512]{2,1,0:T(8,128)(2,1)S(1)}, u32[]{:S(2)}, u32[]{:S(2)}) %all-to-all-start) | async-done | bytes 524320 | tf_op jit(solution)/shard_map/while/body/eval_jaxpr/all_to_all | solution.py:28
  211.2 2.1 copy-done
  213.3 4.5 %conditional.2 = (bf16[64,640]{1,0:T(8,128)(2,1)}, bf16[64,4096]{1,0:T(8,128)(2,1)S(1)}) conditional(s32[]{:T(128)} %convert_element_type.313, () %tuple.49, (bf16[64,4096]{1,0:T(8,128)(2,1)S(1)}, bf16[4096,640]{1,0:T(8,128)(2,1)S(1)}, bf16[640,4096]{1,0:T(8,128)(2,1)}) %tuple.63), branch_computations={%region_2.2_spmd, %region_3.3_spmd} | conditional | flops 671719424 | bytes 32669740 | solution.py:94
  213.3 1.7 fusion.7
  215.0 0.9 copy-done.1
  215.8 1.9 convolution_convert_fusion
  218.0 1.0 copy.67
  218.9 3.5 all-to-all-start.1
  222.4 11.1 %all-to-all-done.1 = bf16[8,64,512]{2,1,0:T(8,128)(2,1)S(1)} async-done(((bf16[8,64,512]{2,1,0:T(8,128)(2,1)}), bf16[8,64,512]{2,1,0:T(8,128)(2,1)S(1)}, u32[]{:S(2)}, u32[]{:S(2)}) %all-to-all-start.1) | async-done | bytes 524320 | tf_op jit(solution)/shard_map/while/body/eval_jaxpr/all_to_all | solution.py:44
  233.7 1.3 collective-permute-start
  235.0 0.9 select_dynamic-update-slice_fusion.5
  236.0 0.8 broadcast_in_dim.44
  236.8 3.5 all-to-all-start
  240.3 12.2 %all-to-all-done = bf16[8,64,512]{2,1,0:T(8,128)(2,1)S(1)} async-done(((bf16[8,64,512]{2,1,0:T(8,128)(2,1)}), bf16[8,64,512]{2,1,0:T(8,128)(2,1)S(1)}, u32[]{:S(2)}, u32[]{:S(2)}) %all-to-all-start) | async-done | bytes 524320 | tf_op jit(solution)/shard_map/while/body/eval_jaxpr/all_to_all | solution.py:28
  253.2 2.1 copy-done
  255.2 0.7 conditional.2
  255.2 0.6 broadcast.38
  256.1 1.0 copy.67
  257.1 3.5 all-to-all-start.1
  260.6 11.1 %all-to-all-done.1 = bf16[8,64,512]{2,1,0:T(8,128)(2,1)S(1)} async-done(((bf16[8,64,512]{2,1,0:T(8,128)(2,1)}), bf16[8,64,512]{2,1,0:T(8,128)(2,1)S(1)}, u32[]{:S(2)}, u32[]{:S(2)}) %all-to-all-start.1) | async-done | bytes 524320 | tf_op jit(solution)/shard_map/while/body/eval_jaxpr/all_to_all | solution.py:44
  271.7 3.6 collective-permute-start
  275.5 0.8 collective-permute-done
  276.3 0.7 copy-done.2
  277.0 0.7 copy.43
  277.7 38.9 %all_to_all.38 = bf16[128,16,256]{0,2,1:T(8,128)(2,1)S(1)} all-to-all(bf16[128,16,256]{0,2,1:T(8,128)(2,1)S(1)} %bitcast.112), channel_id=1, replica_groups=mesh['section'=2,'dp_0'=8,'dp_1'=2,'tensor'=8] {'dp_0','dp_1'}, dimensions={1} | all-to-all | bytes 2097152 | tf_op jit(solution)/shard_map/all_to_all | solution.py:119
  316.5 43.1 %all-gather.9.cloned.1.call-done = bf16[2048,640]{1,0:T(8,128)(2,1)} async-done(((bf16[128,640]{1,0:T(8,128)(2,1)}), bf16[2048,640]{1,0:T(8,128)(2,1)}) %all-gather.9.cloned.1.call-update) | async-done | bytes 2621456 | tf_op jit(solution)/shard_map/all_gather | solution.py:118
  359.7 1.3 convolution_convert_fusion.1
  361.0 1.2 convolution_convert_fusion.2
  362.2 1.2 convolution_convert_fusion.3
  363.4 1.2 convolution_convert_fusion.4
  364.6 1.2 convolution_convert_fusion.5
  365.9 0.3 convolution_convert_fusion.6
  366.1 0.3 convolution_convert_fusion.7
  366.4 0.3 convolution_convert_fusion.8
  366.7 0.3 convolution_convert_fusion.9
  367.0 0.3 convolution_convert_fusion.10
  367.3 0.3 convolution_convert_fusion.11
  367.6 0.3 convolution_convert_fusion.12
  367.9 0.3 convolution_convert_fusion.13
  368.1 0.3 convolution_convert_fusion.14
  368.4 0.3 convolution_convert_fusion.16
  368.7 0.3 convolution_convert_fusion.15
  369.0 1.5 fusion.9
  (60 shorter events, 3.1 us)
Async XLA Ops:
  7.2 21.8 %copy-start.7 = (bf16[1,512]{1,0:T(2,128)(2,1)S(1)}, bf16[1,512]{1,0:T(2,128)(2,1)}, u32[]{:S(2)}) copy-start(bf16[1,512]{1,0:T(2,128)(2,1)} %param.10) | copy-start | bytes 3076
  7.2 144.4 %copy-start.6 = (bf16[128,512]{1,0:T(8,128)(2,1)S(1)}, bf16[128,512]{1,0:T(8,128)(2,1)}, u32[]{:S(2)}) copy-start(bf16[128,512]{1,0:T(8,128)(2,1)} %param.9) | copy-start | bytes 393220
  7.2 79.3 %all-gather.11.cloned.1.call-start = ((), (), s32[]{:S(2)}) async-start(), calls=%async_computation.4 | async-start | bytes 5898240 | tf_op jit(solution)/shard_map/all_gather | solution.py:16
  17.7 133.8 %all-gather.13.cloned.1.call-start = ((), (), s32[]{:S(2)}) async-start(), calls=%async_computation.5 | async-start | bytes 5898240 | tf_op jit(solution)/shard_map/all_gather | solution.py:16
  28.9 330.8 %all-gather.9.cloned.1.call-start = ((), (), s32[]{:S(2)}) async-start(), calls=%async_computation.3 | async-start | bytes 2785280 | tf_op jit(solution)/shard_map/all_gather | solution.py:118
  151.5 125.4 %copy-start.5 = (bf16[1,128,4096]{2,1,0:T(8,128)(2,1)S(1)}, bf16[1,128,4096]{2,1,0:T(8,128)(2,1)}, u32[]{:S(2)}) copy-start(bf16[1,128,4096]{2,1,0:T(8,128)(2,1)} %param.13) | copy-start | bytes 3145732
  152.5 17.2 %all-to-all-start = ((bf16[8,64,512]{2,1,0:T(8,128)(2,1)}), bf16[8,64,512]{2,1,0:T(8,128)(2,1)S(1)}, u32[]{:S(2)}, u32[]{:S(2)}) async-start(bf16[8,64,512]{2,1,0:T(8,128)(2,1)} %broadcast_in_dim.44), calls=%async_computation | async-start | bytes 1048576 | tf_op jit(solution)/shard_map/while/body/eval_jaxpr/all_to_all | solution.py:28
  169.9 2.5 copy-start
  172.4 2.5 copy-start.1
  178.0 13.6 %all-to-all-start.1 = ((bf16[8,64,512]{2,1,0:T(8,128)(2,1)}), bf16[8,64,512]{2,1,0:T(8,128)(2,1)S(1)}, u32[]{:S(2)}, u32[]{:S(2)}) async-start(bf16[8,64,512]{2,1,0:T(8,128)(2,1)} %copy.67), calls=%async_computation.1 | async-start | bytes 1048576 | tf_op jit(solution)/shard_map/while/body/eval_jaxpr/all_to_all | solution.py:44
  191.7 2.2 collective-permute-start
  194.9 15.7 %all-to-all-start = ((bf16[8,64,512]{2,1,0:T(8,128)(2,1)}), bf16[8,64,512]{2,1,0:T(8,128)(2,1)S(1)}, u32[]{:S(2)}, u32[]{:S(2)}) async-start(bf16[8,64,512]{2,1,0:T(8,128)(2,1)} %broadcast_in_dim.44), calls=%async_computation | async-start | bytes 1048576 | tf_op jit(solution)/shard_map/while/body/eval_jaxpr/all_to_all | solution.py:28
  210.8 2.5 copy-start
  213.3 2.5 copy-start.1
  218.9 14.6 %all-to-all-start.1 = ((bf16[8,64,512]{2,1,0:T(8,128)(2,1)}), bf16[8,64,512]{2,1,0:T(8,128)(2,1)S(1)}, u32[]{:S(2)}, u32[]{:S(2)}) async-start(bf16[8,64,512]{2,1,0:T(8,128)(2,1)} %copy.67), calls=%async_computation.1 | async-start | bytes 1048576 | tf_op jit(solution)/shard_map/while/body/eval_jaxpr/all_to_all | solution.py:44
  233.7 2.2 collective-permute-start
  236.8 15.7 %all-to-all-start = ((bf16[8,64,512]{2,1,0:T(8,128)(2,1)}), bf16[8,64,512]{2,1,0:T(8,128)(2,1)S(1)}, u32[]{:S(2)}, u32[]{:S(2)}) async-start(bf16[8,64,512]{2,1,0:T(8,128)(2,1)} %broadcast_in_dim.44), calls=%async_computation | async-start | bytes 1048576 | tf_op jit(solution)/shard_map/while/body/eval_jaxpr/all_to_all | solution.py:28
  252.8 2.5 copy-start
  257.1 14.6 %all-to-all-start.1 = ((bf16[8,64,512]{2,1,0:T(8,128)(2,1)}), bf16[8,64,512]{2,1,0:T(8,128)(2,1)S(1)}, u32[]{:S(2)}, u32[]{:S(2)}) async-start(bf16[8,64,512]{2,1,0:T(8,128)(2,1)} %copy.67), calls=%async_computation.1 | async-start | bytes 1048576 | tf_op jit(solution)/shard_map/while/body/eval_jaxpr/all_to_all | solution.py:44
  271.7 4.5 %collective-permute-start = (bf16[64,512]{1,0:T(8,128)(2,1)S(1)}, bf16[64,512]{1,0:T(8,128)(2,1)S(1)}, u32[]{:S(2)}, u32[]{:S(2)}) collective-permute-start(bf16[64,512]{1,0:T(8,128)(2,1)S(1)} %get-tuple-element.299), channel_id=1, source_target_pairs={{0,128},{1,129},{2,130},{3,131},{4,132},{5,133},{6,134},{7,135},{8... | collective-permute-start | bytes 196616 | tf_op jit(solution)/shard_map/while/body/eval_jaxpr/ppermute | solution.py:51
  276.3 0.7 copy-start.2
  276.3 86.0 %copy-start.4 = (bf16[128,512]{1,0:T(8,128)(2,1)}, bf16[128,512]{1,0:T(8,128)(2,1)S(1)}, u32[]{:S(2)}) copy-start(bf16[128,512]{1,0:T(8,128)(2,1)S(1)} %get-tuple-element.209) | copy-start | bytes 393220
  359.7 6.2 %copy-start.3 = (bf16[2048,640]{1,0:T(8,128)(2,1)S(1)}, bf16[2048,640]{1,0:T(8,128)(2,1)}, u32[]{:S(2)}) copy-start(bf16[2048,640]{1,0:T(8,128)(2,1)} %all-gather.9.cloned.1.call-done) | copy-start | bytes 7864324
Sparse Core Ops, SparseCore 0:
  17.8 68.6 all-gather.10
  88.3 63.1 all-gather.12
  277.1 82.5 all-gather.8
where the time goes:
time: 378 us; the launch traced here: 377 us
  waiting for transfers between devices  203 us (54%)
  blocking collectives  92.1 us (24%)
  starting transfers between devices  29.6 us (8%)
  matrix products  16.4 us (4%)
  local copies, waits for them, and re-layouts  16.2 us (4%)
  between operations  14 us (4%)
  other arithmetic  5.33 us (1%)
    all_gather x2, waiting for transfers between devices, gathered_by_axis(): filled = lax.all_gather(filled, axes[number], axis=dim, tiled=True)  90.9 us
    all_gather x1, waiting for transfers between devices, body(): hidden_all = lax.all_gather(hiddens, DP, axis=0, tiled=True)  43.1 us
    all_to_all x1, blocking collectives, body(): lax.all_to_all(cot_own, DP, split_axis=1, concat_axis=0, tiled=True)  38.9 us
    all_to_all x3, waiting for transfers between devices, copy_for_each(): lax.all_to_all(jnp.broadcast_to(array[None], (peers, *array.shape)), axis...  35.8 us
    all_to_all x3, waiting for transfers between devices, summed_on_arrival(): lax.all_to_all(pieces, axis, split_axis=0, concat_axis=0, tiled=True)  32.3 us
    all_gather x1, blocking collectives, body(): gain_whole = lax.all_gather(gain_own, 'tensor', axis=0, tiled=True)  31.6 us
    all_gather x2, blocking collectives, gathered_by_axis(): filled = lax.all_gather(filled, axes[number], axis=dim, tiled=True)  21.6 us
    all_to_all x3, starting transfers between devices, copy_for_each(): lax.all_to_all(jnp.broadcast_to(array[None], (peers, *array.shape)), axis...  12.8 us
  transfers between devices with their start and end apart: 12, of which 10 were waited for; matrix products, arithmetic and copies ran while one was open for 1% of the time, Pallas kernels for 0%

commit v1 on v0

--- a/solution.py
+++ b/solution.py
@@ -115,7 +115,9 @@
     hiddens = final_state[2]
     cot_own = cotangent[0]
     dp_count = lax.axis_size(DP)
-    hidden_all = lax.all_gather(hiddens, DP, axis=0, tiled=True)
+    hidden_all = jnp.concatenate(
+        lax.all_to_all(jnp.stack([hiddens] * lax.axis_size(DP)), DP, 0, 0), axis=0
+    )
     cot_mine = lax.all_to_all(cot_own, DP, split_axis=1, concat_axis=0, tiled=True)
     grad_own = jnp.zeros((hidden_width, width // dp_count), jnp.float32)
     for peer_id in range(dp_count):

time: 378 us -> 381 us (level)
  waiting for transfers between devices: 203 us -> 171 us
  blocking collectives: 92.1 us -> 120 us
  starting transfers between devices: 29.6 us -> 40.1 us
  matrix products: 16.4 us -> 11.7 us
    all_gather x1 -> x0, waiting for transfers between devices: 43.1 us -> none  [body(): hidden_all = lax.all_gather(hiddens, DP, axis=0, tiled=True)]
    all_to_all x1, blocking collectives: 38.9 us -> 67.5 us  [body(): lax.all_to_all(jnp.stack([hiddens] * lax.axis_size(DP)), DP, 0, 0)]
    all_to_all x0 -> x1, starting transfers between devices: none -> 10.5 us  [body(): lax.all_to_all(cot_own, DP, split_axis=1, concat_axis=0, tiled=True)]
    all_to_all x0 -> x1, waiting for transfers between devices: none -> 6.2 us  [body(): lax.all_to_all(cot_own, DP, split_axis=1, concat_axis=0, tiled=True)]
    all_gather x2, waiting for transfers between devices: 90.9 us -> 95.8 us  [gathered_by_axis(): filled = lax.all_gather(filled, axes[number], axis=dim, tiled=True)]
    dot_general x16, matrix products: 9.16 us -> 4.46 us  [body(): lax.dot_general(hidden_all[lower:lower + tok_rows], cot_mine[lower:lower...]
where the time goes in v1:
time: 381 us; the launch traced here: 379 us
  waiting for transfers between devices  171 us (45%)
  blocking collectives  120 us (31%)
  starting transfers between devices  40.1 us (11%)
  local copies, waits for them, and re-layouts  16.5 us (4%)
  between operations  14.2 us (4%)
  matrix products  11.7 us (3%)
  other arithmetic  5.25 us (1%)
    all_gather x2, waiting for transfers between devices, gathered_by_axis(): filled = lax.all_gather(filled, axes[number], axis=dim, tiled=True)  95.8 us
    all_to_all x1, blocking collectives, body(): lax.all_to_all(jnp.stack([hiddens] * lax.axis_size(DP)), DP, 0, 0)  67.5 us
    all_to_all x3, waiting for transfers between devices, copy_for_each(): lax.all_to_all(jnp.broadcast_to(array[None], (peers, *array.shape)), axis...  35.8 us
    all_to_all x3, waiting for transfers between devices, summed_on_arrival(): lax.all_to_all(pieces, axis, split_axis=0, concat_axis=0, tiled=True)  32.3 us
    all_gather x1, blocking collectives, body(): gain_whole = lax.all_gather(gain_own, 'tensor', axis=0, tiled=True)  31.1 us
    all_gather x2, blocking collectives, gathered_by_axis(): filled = lax.all_gather(filled, axes[number], axis=dim, tiled=True)  21.7 us
    all_to_all x3, starting transfers between devices, copy_for_each(): lax.all_to_all(jnp.broadcast_to(array[None], (peers, *array.shape)), axis...  12.8 us
    all_to_all x1, starting transfers between devices, body(): lax.all_to_all(cot_own, DP, split_axis=1, concat_axis=0, tiled=True)  10.5 us
  transfers between devices with their start and end apart: 12, of which 10 were waited for; matrix products, arithmetic and copies ran while one was open for 1% of the time, Pallas kernels for 0%

profile of v1, /device:TPU:2, one launch (start us, length us, event | category | flops | bytes accessed | tf_op | source)
XLA Modules:
  0.0 379.5 jit_solution(14249435148735154991)
XLA Ops:
  7.2 10.6 %all-gather.1 = bf16[1,512,640]{2,1,0:T(8,128)(2,1)} all-gather(bf16[1,256,640]{2,1,0:T(8,128)(2,1)} %param.11), channel_id=3, replica_groups=mesh['section'=2,'dp_0'=8,'dp_1'=2,'tensor'=8] {'dp_1'}, dimensions={1}, use_global_device_ids=true | all-gather | bytes 983040 | tf_op jit(solution)/shard_map/all_gather | solution.py:16
  17.9 11.1 %all-gather.3 = bf16[1,640,512]{2,1,0:T(8,128)(2,1)} all-gather(bf16[1,640,256]{2,1,0:T(8,128)(2,1)} %param.12), channel_id=5, replica_groups=mesh['section'=2,'dp_0'=8,'dp_1'=2,'tensor'=8] {'dp_1'}, dimensions={2}, use_global_device_ids=true | all-gather | bytes 983040 | tf_op jit(solution)/shard_map/all_gather | solution.py:16
  29.0 1.3 copy.43
  30.3 10.5 %all-to-all-start.3 = ((bf16[128,16,256]{0,2,1:T(8,128)(2,1)}), bf16[128,16,256]{0,2,1:T(8,128)(2,1)S(1)}, u32[]{:S(2)}, u32[]{:S(2)}) async-start(bf16[128,16,256]{0,2,1:T(8,128)(2,1)} %bitcast.6), calls=%async_computation.3 | async-start | bytes 2097152 | tf_op jit(solution)/shard_map/all_to_all | solution.py:121
  40.9 31.1 %all-gather = bf16[1,4096]{1,0:T(2,128)(2,1)S(1)} all-gather(bf16[1,512]{1,0:T(2,128)(2,1)S(1)} %copy-done.5), channel_id=2, replica_groups=mesh['section'=2,'dp_0'=8,'dp_1'=2,'tensor'=8] {'tensor'}, dimensions={1}, use_global_device_ids=true | all-gather | bytes 9216 | tf_op jit(solution)/shard_map/all_gather | solution.py:62
  72.1 6.2 %all-to-all-done.3 = bf16[128,16,256]{0,2,1:T(8,128)(2,1)S(1)} async-done(((bf16[128,16,256]{0,2,1:T(8,128)(2,1)}), bf16[128,16,256]{0,2,1:T(8,128)(2,1)S(1)}, u32[]{:S(2)}, u32[]{:S(2)}) %all-to-all-start.3) | async-done | bytes 1048608 | tf_op jit(solution)/shard_map/all_to_all | solution.py:121
  78.3 30.8 %all-gather.8.cloned.1.call-done = bf16[1,4096,640]{2,1,0:T(8,128)(2,1)} async-done(((bf16[1,512,640]{2,1,0:T(8,128)(2,1)}), bf16[1,4096,640]{2,1,0:T(8,128)(2,1)}) %all-gather.8.cloned.1.call-update) | async-done | bytes 5242896 | tf_op jit(solution)/shard_map/all_gather | solution.py:16
  109.1 65.0 %all-gather.10.cloned.1.call-done = bf16[1,640,4096]{2,1,0:T(8,128)(2,1)} async-done(((bf16[1,640,512]{2,1,0:T(8,128)(2,1)}), bf16[1,640,4096]{2,1,0:T(8,128)(2,1)}) %all-gather.10.cloned.1.call-update) | async-done | bytes 5242896 | tf_op jit(solution)/shard_map/all_gather | solution.py:16
  174.1 124.7 %while.18 = (s32[]{:T(128)}, bf16[64,512]{1,0:T(8,128)(2,1)S(1)}, bf16[128,512]{1,0:T(8,128)(2,1)S(1)}, bf16[128,640]{1,0:T(8,128)(2,1)S(1)}, pred[]{:T(512)}, /...) while((s32[]{:T(128)}, bf16[64,512]{1,0:T(8,128)(2,1)S(1)}, ...), condition=%wide.region_5.6_spmd, body=%wide.region_0.5_spmd.sunk | while | flops 674254912 | bytes 67036620 | solution.py:113
  174.2 0.8 broadcast_in_dim.44
  175.0 5.8 %all-to-all-start = ((bf16[8,64,512]{2,1,0:T(8,128)(2,1)}), bf16[8,64,512]{2,1,0:T(8,128)(2,1)S(1)}, u32[]{:S(2)}, u32[]{:S(2)}) async-start(bf16[8,64,512]{2,1,0:T(8,128)(2,1)} %broadcast_in_dim.44), calls=%async_computation | async-start | bytes 1048576 | tf_op jit(solution)/shard_map/while/body/eval_jaxpr/all_to_all | solution.py:28
  180.9 11.4 %all-to-all-done = bf16[8,64,512]{2,1,0:T(8,128)(2,1)S(1)} async-done(((bf16[8,64,512]{2,1,0:T(8,128)(2,1)}), bf16[8,64,512]{2,1,0:T(8,128)(2,1)S(1)}, u32[]{:S(2)}, u32[]{:S(2)}) %all-to-all-start) | async-done | bytes 524320 | tf_op jit(solution)/shard_map/while/body/eval_jaxpr/all_to_all | solution.py:28
  192.9 2.1 copy-done
  195.0 4.5 %conditional.2 = (bf16[64,640]{1,0:T(8,128)(2,1)}, bf16[64,4096]{1,0:T(8,128)(2,1)S(1)}) conditional(s32[]{:T(128)} %convert_element_type.313, () %tuple.49, (bf16[64,4096]{1,0:T(8,128)(2,1)S(1)}, bf16[4096,640]{1,0:T(8,128)(2,1)S(1)}, bf16[640,4096]{1,0:T(8,128)(2,1)}) %tuple.61), branch_computations={%region_2.2_spmd, %region_3.3_spmd} | conditional | flops 671719424 | bytes 32669740 | solution.py:94
  195.0 1.7 fusion.7
  196.6 0.8 copy-done.1
  197.5 1.9 convolution_convert_fusion
  199.6 1.0 copy.67
  200.6 3.5 all-to-all-start.1
  204.1 10.1 %all-to-all-done.1 = bf16[8,64,512]{2,1,0:T(8,128)(2,1)S(1)} async-done(((bf16[8,64,512]{2,1,0:T(8,128)(2,1)}), bf16[8,64,512]{2,1,0:T(8,128)(2,1)S(1)}, u32[]{:S(2)}, u32[]{:S(2)}) %all-to-all-start.1) | async-done | bytes 524320 | tf_op jit(solution)/shard_map/while/body/eval_jaxpr/all_to_all | solution.py:44
  214.3 1.3 collective-permute-start
  215.6 0.9 select_dynamic-update-slice_fusion.5
  216.6 0.8 broadcast_in_dim.44
  217.5 3.5 all-to-all-start
  221.0 12.2 %all-to-all-done = bf16[8,64,512]{2,1,0:T(8,128)(2,1)S(1)} async-done(((bf16[8,64,512]{2,1,0:T(8,128)(2,1)}), bf16[8,64,512]{2,1,0:T(8,128)(2,1)S(1)}, u32[]{:S(2)}, u32[]{:S(2)}) %all-to-all-start) | async-done | bytes 524320 | tf_op jit(solution)/shard_map/while/body/eval_jaxpr/all_to_all | solution.py:28
  233.8 2.1 copy-done
  235.9 4.5 %conditional.2 = (bf16[64,640]{1,0:T(8,128)(2,1)}, bf16[64,4096]{1,0:T(8,128)(2,1)S(1)}) conditional(s32[]{:T(128)} %convert_element_type.313, () %tuple.49, (bf16[64,4096]{1,0:T(8,128)(2,1)S(1)}, bf16[4096,640]{1,0:T(8,128)(2,1)S(1)}, bf16[640,4096]{1,0:T(8,128)(2,1)}) %tuple.61), branch_computations={%region_2.2_spmd, %region_3.3_spmd} | conditional | flops 671719424 | bytes 32669740 | solution.py:94
  235.9 1.7 fusion.7
  237.6 0.9 copy-done.1
  238.4 1.9 convolution_convert_fusion
  240.6 1.0 copy.67
  241.5 3.5 all-to-all-start.1
  245.0 11.1 %all-to-all-done.1 = bf16[8,64,512]{2,1,0:T(8,128)(2,1)S(1)} async-done(((bf16[8,64,512]{2,1,0:T(8,128)(2,1)}), bf16[8,64,512]{2,1,0:T(8,128)(2,1)S(1)}, u32[]{:S(2)}, u32[]{:S(2)}) %all-to-all-start.1) | async-done | bytes 524320 | tf_op jit(solution)/shard_map/while/body/eval_jaxpr/all_to_all | solution.py:44
  256.2 1.3 collective-permute-start
  257.5 0.9 select_dynamic-update-slice_fusion.5
  258.5 0.8 broadcast_in_dim.44
  259.4 3.5 all-to-all-start
  262.9 12.2 %all-to-all-done = bf16[8,64,512]{2,1,0:T(8,128)(2,1)S(1)} async-done(((bf16[8,64,512]{2,1,0:T(8,128)(2,1)}), bf16[8,64,512]{2,1,0:T(8,128)(2,1)S(1)}, u32[]{:S(2)}, u32[]{:S(2)}) %all-to-all-start) | async-done | bytes 524320 | tf_op jit(solution)/shard_map/while/body/eval_jaxpr/all_to_all | solution.py:28
  275.7 2.1 copy-done
  277.8 0.7 conditional.2
  277.8 0.6 broadcast.40
  278.7 1.0 copy.67
  279.6 3.5 all-to-all-start.1
  283.1 11.1 %all-to-all-done.1 = bf16[8,64,512]{2,1,0:T(8,128)(2,1)S(1)} async-done(((bf16[8,64,512]{2,1,0:T(8,128)(2,1)}), bf16[8,64,512]{2,1,0:T(8,128)(2,1)S(1)}, u32[]{:S(2)}, u32[]{:S(2)}) %all-to-all-start.1) | async-done | bytes 524320 | tf_op jit(solution)/shard_map/while/body/eval_jaxpr/all_to_all | solution.py:44
  294.3 3.6 collective-permute-start
  298.0 0.8 collective-permute-done
  298.9 0.3 stack.2
  299.2 67.5 %all_to_all.43 = bf16[16,128,640]{2,1,0:T(8,128)(2,1)S(1)} all-to-all(bf16[16,128,640]{2,1,0:T(8,128)(2,1)S(1)} %stack.2), channel_id=1, replica_groups=mesh['section'=2,'dp_0'=8,'dp_1'=2,'tensor'=8] {'dp_0','dp_1'}, dimensions={0} | all-to-all | bytes 5242880 | tf_op jit(solution)/shard_map/all_to_all | solution.py:119
  366.7 0.3 convolution_convert_fusion.1
  366.9 0.3 convolution_convert_fusion.2
  367.2 0.3 convolution_convert_fusion.3
  367.5 0.3 convolution_convert_fusion.4
  367.8 0.3 convolution_convert_fusion.5
  368.1 0.3 convolution_convert_fusion.6
  368.4 0.3 convolution_convert_fusion.7
  368.7 0.3 convolution_convert_fusion.8
  368.9 0.3 convolution_convert_fusion.9
  369.2 0.3 convolution_convert_fusion.10
  369.5 0.3 convolution_convert_fusion.11
  369.8 0.3 convolution_convert_fusion.12
  370.1 0.3 convolution_convert_fusion.13
  370.4 0.3 convolution_convert_fusion.14
  370.7 0.3 convolution_convert_fusion.16
  371.2 1.4 fusion.9
  (56 shorter events, 3.3 us)
Async XLA Ops:
  7.2 21.9 %copy-start.3 = (bf16[1,128,4096]{2,1,0:T(8,128)(2,1)S(1)}, bf16[1,128,4096]{2,1,0:T(8,128)(2,1)}, u32[]{:S(2)}) copy-start(bf16[1,128,4096]{2,1,0:T(8,128)(2,1)} %param.13) | copy-start | bytes 3145732
  7.2 101.9 %all-gather.8.cloned.1.call-start = ((), (), s32[]{:S(2)}) async-start(), calls=%async_computation.4 | async-start | bytes 5898240 | tf_op jit(solution)/shard_map/all_gather | solution.py:16
  17.8 156.3 %all-gather.10.cloned.1.call-start = ((), (), s32[]{:S(2)}) async-start(), calls=%async_computation.5 | async-start | bytes 5898240 | tf_op jit(solution)/shard_map/all_gather | solution.py:16
  29.0 11.9 %copy-start.5 = (bf16[1,512]{1,0:T(2,128)(2,1)S(1)}, bf16[1,512]{1,0:T(2,128)(2,1)}, u32[]{:S(2)}) copy-start(bf16[1,512]{1,0:T(2,128)(2,1)} %param.10) | copy-start | bytes 3076
  29.0 145.1 %copy-start.4 = (bf16[128,512]{1,0:T(8,128)(2,1)S(1)}, bf16[128,512]{1,0:T(8,128)(2,1)}, u32[]{:S(2)}) copy-start(bf16[128,512]{1,0:T(8,128)(2,1)} %param.9) | copy-start | bytes 393220
  30.3 47.9 %all-to-all-start.3 = ((bf16[128,16,256]{0,2,1:T(8,128)(2,1)}), bf16[128,16,256]{0,2,1:T(8,128)(2,1)S(1)}, u32[]{:S(2)}, u32[]{:S(2)}) async-start(bf16[128,16,256]{0,2,1:T(8,128)(2,1)} %bitcast.6), calls=%async_computation.3 | async-start | bytes 2097152 | tf_op jit(solution)/shard_map/all_to_all | solution.py:121
  175.0 17.2 %all-to-all-start = ((bf16[8,64,512]{2,1,0:T(8,128)(2,1)}), bf16[8,64,512]{2,1,0:T(8,128)(2,1)S(1)}, u32[]{:S(2)}, u32[]{:S(2)}) async-start(bf16[8,64,512]{2,1,0:T(8,128)(2,1)} %broadcast_in_dim.44), calls=%async_computation | async-start | bytes 1048576 | tf_op jit(solution)/shard_map/while/body/eval_jaxpr/all_to_all | solution.py:28
  192.5 2.5 copy-start
  195.0 2.5 copy-start.1
  200.6 13.6 %all-to-all-start.1 = ((bf16[8,64,512]{2,1,0:T(8,128)(2,1)}), bf16[8,64,512]{2,1,0:T(8,128)(2,1)S(1)}, u32[]{:S(2)}, u32[]{:S(2)}) async-start(bf16[8,64,512]{2,1,0:T(8,128)(2,1)} %copy.67), calls=%async_computation.1 | async-start | bytes 1048576 | tf_op jit(solution)/shard_map/while/body/eval_jaxpr/all_to_all | solution.py:44
  214.3 2.2 collective-permute-start
  217.5 15.7 %all-to-all-start = ((bf16[8,64,512]{2,1,0:T(8,128)(2,1)}), bf16[8,64,512]{2,1,0:T(8,128)(2,1)S(1)}, u32[]{:S(2)}, u32[]{:S(2)}) async-start(bf16[8,64,512]{2,1,0:T(8,128)(2,1)} %broadcast_in_dim.44), calls=%async_computation | async-start | bytes 1048576 | tf_op jit(solution)/shard_map/while/body/eval_jaxpr/all_to_all | solution.py:28
  233.4 2.5 copy-start
  235.9 2.5 copy-start.1
  241.5 14.6 %all-to-all-start.1 = ((bf16[8,64,512]{2,1,0:T(8,128)(2,1)}), bf16[8,64,512]{2,1,0:T(8,128)(2,1)S(1)}, u32[]{:S(2)}, u32[]{:S(2)}) async-start(bf16[8,64,512]{2,1,0:T(8,128)(2,1)} %copy.67), calls=%async_computation.1 | async-start | bytes 1048576 | tf_op jit(solution)/shard_map/while/body/eval_jaxpr/all_to_all | solution.py:44
  256.2 2.2 collective-permute-start
  259.4 15.7 %all-to-all-start = ((bf16[8,64,512]{2,1,0:T(8,128)(2,1)}), bf16[8,64,512]{2,1,0:T(8,128)(2,1)S(1)}, u32[]{:S(2)}, u32[]{:S(2)}) async-start(bf16[8,64,512]{2,1,0:T(8,128)(2,1)} %broadcast_in_dim.44), calls=%async_computation | async-start | bytes 1048576 | tf_op jit(solution)/shard_map/while/body/eval_jaxpr/all_to_all | solution.py:28
  275.3 2.5 copy-start
  279.6 14.6 %all-to-all-start.1 = ((bf16[8,64,512]{2,1,0:T(8,128)(2,1)}), bf16[8,64,512]{2,1,0:T(8,128)(2,1)S(1)}, u32[]{:S(2)}, u32[]{:S(2)}) async-start(bf16[8,64,512]{2,1,0:T(8,128)(2,1)} %copy.67), calls=%async_computation.1 | async-start | bytes 1048576 | tf_op jit(solution)/shard_map/while/body/eval_jaxpr/all_to_all | solution.py:44
  294.3 4.5 %collective-permute-start = (bf16[64,512]{1,0:T(8,128)(2,1)S(1)}, bf16[64,512]{1,0:T(8,128)(2,1)S(1)}, u32[]{:S(2)}, u32[]{:S(2)}) collective-permute-start(bf16[64,512]{1,0:T(8,128)(2,1)S(1)} %get-tuple-element.299), channel_id=1, source_target_pairs={{0,128},{1,129},{2,130},{3,131},{4,132},{5,133},{6,134},{7,135},{8... | collective-permute-start | bytes 196616 | tf_op jit(solution)/shard_map/while/body/eval_jaxpr/ppermute | solution.py:51
  298.9 67.8 %copy-start.2 = (bf16[128,512]{1,0:T(8,128)(2,1)}, bf16[128,512]{1,0:T(8,128)(2,1)S(1)}, u32[]{:S(2)}) copy-start(bf16[128,512]{1,0:T(8,128)(2,1)S(1)} %get-tuple-element.209) | copy-start | bytes 393220
Sparse Core Ops, SparseCore 0:
  17.9 91.0 all-gather.7
  110.9 63.1 all-gather.9
